TPU v7x, 8 devices: a whole 2x2x1 slice. The times are simulated.
8 devices in a mesh: ens: 2 (over z, y), sp: 4 (over x, core).
Axes of the slice: x: 2, y: 2, z: 1, core: 2. Of those that a mesh axis runs over, the one named last changes fastest.
Arguments:
- x_seq: bfloat16 [4096, 512], P(('ens', 'sp')), parts along dimension 0
- w_past: bfloat16 [3, 10, 512, 1024], replicated
- w_now: bfloat16 [3, 10, 512, 1024], replicated
- b_conv: float32 [3, 10, 1024], replicated
- w_res: bfloat16 [3, 10, 512, 512], replicated
- w_skip: bfloat16 [3, 10, 512, 256], replicated
- w_out1: bfloat16 [256, 256], replicated
- b_out1: float32 [256], replicated
- w_out2: bfloat16 [256, 256], replicated
- b_out2: float32 [256], replicated
Outputs:
- output 1: float32 [4096, 256], P(('ens', 'sp')), parts along dimension 0
- output 2: bfloat16 [4096, 512], P(('ens', 'sp')), parts along dimension 0
There are 2 independent parts. A program takes and returns all parts, laid end to end along the dimension named above; an argument that names none is the same for every part.
All inputs are finite; a program needn't handle non-finite values.
Results may differ from a plain program's by a relative error of at most 0.02.
Values are sent between devices in bfloat16 or wider.
A program may use at most 1 GiB of HBM per device.

v0:
```python
import functools

import jax
import jax.numpy as jnp
from jax import lax
from jax.experimental import pallas as pl
from jax.experimental.pallas import tpu as pltpu
from jax.sharding import PartitionSpec as P

TILE = 16
SLOTS = 5
STATIC = 4


def _kernel(n_sp, repeats, cycle, rows, x_ref, wp_ref, wn_ref, b_ref, wr_ref, ws_ref, w1_ref, c1_ref, w2_ref, c2_ref,
            y_ref, h_ref, hb, g_s, skip, wpb, wnb, wrb, wsb, wsem, xsem, osem, send_sem, recv_sem):
    me = lax.axis_index("sp")
    layers = repeats * cycle
    ch = x_ref.shape[1]
    gate = wn_ref.shape[2] // 2
    pads = [max(TILE, 2 ** k) for k in range(cycle)]
    stack_rows = sum(pads) + cycle * rows

    def base_of(s, k):
        return s * stack_rows + sum(pads[:k]) + k * rows

    def weight_copies(layer, slot):
        pairs = ((wp_ref, wpb), (wn_ref, wnb), (wr_ref, wrb), (ws_ref, wsb))
        return [pltpu.make_async_copy(src.at[layer], dst.at[slot], wsem.at[slot, i]) for i, (src, dst) in enumerate(pairs)]

    def halo_copy(s, base, k, pad):
        return pltpu.make_async_remote_copy(
            src_ref=hb.at[pl.ds(pl.multiple_of(base + rows, TILE), pad), :],
            dst_ref=hb.at[pl.ds(pl.multiple_of(base, TILE), pad), :],
            send_sem=send_sem.at[s, k], recv_sem=recv_sem.at[s, k],
            device_id={"sp": jnp.minimum(me + 1, n_sp - 1)}, device_id_type=pl.DeviceIdType.MESH)

    x_copy = pltpu.make_async_copy(x_ref, hb.at[pl.ds(pads[0], rows), :], xsem)
    x_copy.start()
    for slot in range(SLOTS - 1):
        for c in weight_copies(slot, slot):
            c.start()
    barrier = pltpu.get_barrier_semaphore()

    @pl.when(me > 0)
    def _():
        pl.semaphore_signal(barrier, inc=1, device_id={"sp": me - 1}, device_id_type=pl.DeviceIdType.MESH)

    @pl.when(me == 0)
    def _():
        for s in range(repeats):
            for k in range(cycle):
                hb[base_of(s, k):base_of(s, k) + pads[k], :] = jnp.zeros((pads[k], ch), hb.dtype)

    skip[...] = jnp.zeros_like(skip)

    @pl.when(me < n_sp - 1)
    def _():
        pl.semaphore_wait(barrier, 1)

    x_copy.wait()

    def layer_body(s, k, base, pad, next_local, static_d):
        layer = s * cycle + k
        slot = lax.rem(layer, SLOTS)
        local = pl.multiple_of(base + pad, TILE)
        if static_d is not None:
            @pl.when(me < n_sp - 1)
            def _():
                halo_copy(s, base, k, TILE).start()
        else:
            for kk in range(STATIC, cycle):
                @pl.when((me < n_sp - 1) & (k == kk))
                def _():
                    halo_copy(s, base, k, pads[kk]).start()
        ahead = layer + SLOTS - 1

        @pl.when(ahead < layers)
        def _():
            for c in weight_copies(ahead, lax.rem(ahead, SLOTS)):
                c.start()
        for c in weight_copies(layer, slot):
            c.wait()
        if static_d is not None:
            @pl.when(me > 0)
            def _():
                halo_copy(s, base, k, TILE).wait_recv()
        else:
            for kk in range(STATIC, cycle):
                @pl.when((me > 0) & (k == kk))
                def _():
                    halo_copy(s, base, k, pads[kk]).wait_recv()
        here = hb[pl.ds(local, rows), :]
        if static_d is not None:
            past = hb[pl.ds(local - TILE, rows + TILE), :][TILE - static_d:TILE - static_d + rows, :]
        else:
            past = hb[pl.ds(pl.multiple_of(base, TILE), rows), :]
        half = gate // 2
        for j in range(2):
            def pre(col):
                return (jnp.dot(past, wpb[slot, :, col:col + half], preferred_element_type=jnp.float32)
                        + jnp.dot(here, wnb[slot, :, col:col + half], preferred_element_type=jnp.float32)
                        + b_ref[pl.ds(layer, 1), col:col + half])
            a = jnp.tanh(pre(j * half))
            t = jnp.tanh(0.5 * pre(gate + j * half))
            g_s[:, j * half:(j + 1) * half] = (a * (0.5 * t + 0.5)).astype(jnp.bfloat16)
        g = g_s[...]
        new = here.astype(jnp.float32) + jnp.dot(g, wrb[slot], preferred_element_type=jnp.float32)
        hb[pl.ds(pl.multiple_of(next_local, TILE), rows), :] = new.astype(hb.dtype)
        skip[...] += jnp.dot(g, wsb[slot], preferred_element_type=jnp.float32)

    def stack(s, carry):
        for k in range(STATIC):
            nxt = base_of(s, k + 1) + pads[k + 1]
            layer_body(s, k, base_of(s, k), pads[k], nxt, 2 ** k)

        def wide(k, carry):
            base, pad = carry
            last = k == cycle - 1
            next_base = base + pad + rows
            next_pad = jnp.where(last, pads[0], 2 * pad)
            layer_body(s, k, base, pad, next_base + next_pad, None)
            return next_base, next_pad

        lax.fori_loop(STATIC, cycle, wide, (base_of(s, STATIC), jnp.int32(pads[STATIC])))
        return carry

    lax.fori_loop(0, repeats, stack, 0)

    final = repeats * stack_rows + pads[0]
    out_copy = pltpu.make_async_copy(hb.at[pl.ds(final, rows), :], h_ref, osem)
    out_copy.start()
    act = jnp.maximum(skip[...], 0.0).astype(jnp.bfloat16)
    mid = jnp.dot(act, w1_ref[...], preferred_element_type=jnp.float32) + c1_ref[...]
    mid = jnp.maximum(mid, 0.0).astype(jnp.bfloat16)
    y_ref[...] = jnp.dot(mid, w2_ref[...], preferred_element_type=jnp.float32) + c2_ref[...]
    out_copy.wait()

    @pl.when(me < n_sp - 1)
    def _():
        for s in range(repeats):
            for k in range(cycle):
                halo_copy(s, base_of(s, k), k, pads[k]).wait_send()


def solution(mesh):
    n_sp = mesh.shape["sp"]
    row_spec = P(("ens", "sp"), None)

    def local_stack(x_seq, w_past, w_now, b_conv, w_res, w_skip, w_out1, b_out1, w_out2, b_out2):
        repeats, cycle, ch, wide = w_past.shape
        layers, rows = repeats * cycle, x_seq.shape[0]
        gate, skips = w_res.shape[2], w_skip.shape[3]
        classes = w_out2.shape[1]
        pads = [max(TILE, 2 ** k) for k in range(cycle)]
        region = repeats * (sum(pads) + cycle * rows) + pads[0] + rows
        hbm = pl.BlockSpec(memory_space=pltpu.HBM)
        vmem = pl.BlockSpec(memory_space=pltpu.VMEM)
        return pl.pallas_call(
            functools.partial(_kernel, n_sp, repeats, cycle, rows),
            name="stack",
            out_shape=(jax.ShapeDtypeStruct((rows, classes), jnp.float32), jax.ShapeDtypeStruct((rows, ch), x_seq.dtype)),
            in_specs=[hbm, hbm, hbm, vmem, hbm, hbm, vmem, vmem, vmem, vmem],
            out_specs=(vmem, hbm),
            scratch_shapes=[
                pltpu.VMEM((region, ch), x_seq.dtype),
                pltpu.VMEM((rows, gate), jnp.bfloat16),
                pltpu.VMEM((rows, skips), jnp.float32),
                pltpu.VMEM((SLOTS, ch, wide), w_past.dtype),
                pltpu.VMEM((SLOTS, ch, wide), w_now.dtype),
                pltpu.VMEM((SLOTS, gate, ch), w_res.dtype),
                pltpu.VMEM((SLOTS, gate, skips), w_skip.dtype),
                pltpu.SemaphoreType.DMA((SLOTS, 4)),
                pltpu.SemaphoreType.DMA,
                pltpu.SemaphoreType.DMA,
                pltpu.SemaphoreType.DMA((repeats, cycle)),
                pltpu.SemaphoreType.DMA((repeats, cycle)),
            ],
            compiler_params=pltpu.CompilerParams(collective_id=0, has_side_effects=True, vmem_limit_bytes=60 * 2 ** 20),
        )(x_seq, w_past.reshape(layers, ch, wide), w_now.reshape(layers, ch, wide), b_conv.reshape(layers, wide),
          w_res.reshape(layers, gate, ch), w_skip.reshape(layers, gate, skips),
          w_out1, b_out1.reshape(1, -1), w_out2, b_out2.reshape(1, -1))

    return jax.shard_map(
        local_stack,
        mesh=mesh,
        in_specs=(row_spec, P(), P(), P(), P(), P(), P(), P(), P(), P()),
        out_specs=(row_spec, row_spec),
        check_vma=False,
    )
```

profile of v0, /device:TPU:7, one launch (start us, length us, event | category | flops | bytes accessed | tf_op | source)
XLA Modules:
  0.0 80.3 jit_solution(16322962225883973894)
XLA Ops:
  0.6 1.0 %copy.13 = f32[3,10,1024]{2,1,0:T(8,128)S(1)} copy(f32[3,10,1024]{2,0,1:T(4,128)} %param.13) | data formatting | bytes 245760 | tf_op args[3]
  1.6 0.7 reshape.27.b_ref
  2.3 74.3 %stack.1 = (f32[512,256]{1,0:T(8,128)}, bf16[512,512]{1,0:T(8,128)(2,1)}) custom-call(bf16[512,512]{1,0:T(8,128)(2,1)} %x_ref.1, bf16[30,512,1024]{2,1,0:T(8,128)(2,1)} %bitcast.6, bf16[30,512,1024]{2,1,0:T(8,128)(2,1)} %bitcast.7, f32[30,1024]{1,0:T(8,128)} %reshape.27.b_ref, bf16[30,512,512]{2,1,0:T(8,128)(2,1)} %bitcast.8, bf16[30,512,256]{2,1,0:T(8,128)(2,1)} %bitcast.9, ...), custom_call_target="tpu_custom_call" | custom-call | tf_op jit(solution)/shard_map/stack/pallas_call | solution.py:159
  76.6 1.9 %copy.16 = f32[512,256]{1,0:T(8,128)} copy(f32[512,256]{1,0:T(8,128)} %get-tuple-element.4) | data formatting | bytes 1048576
  78.4 1.9 %copy.17 = bf16[512,512]{1,0:T(8,128)(2,1)} copy(bf16[512,512]{1,0:T(8,128)(2,1)} %get-tuple-element.5) | data formatting | bytes 1048576
where the time goes:
time: 80.5 us; the launch traced here: 80.3 us
  Pallas kernels  74.3 us (92%)
  local copies, waits for them, and re-layouts  5.4 us (7%)
    pallas_call x1, Pallas kernels, local_stack(): pl.pallas_call(functools.partial(_kernel, n_sp, repeats, cycle, rows), na...  74.3 us
    unnamed x3, local copies, waits for them, and re-layouts  4.73 us

commit v1 on v0

v1 whole, which is shorter than its diff:
```python
import functools

import jax
import jax.numpy as jnp
from jax import lax
from jax.experimental import pallas as pl
from jax.experimental.pallas import tpu as pltpu
from jax.sharding import PartitionSpec as P

TILE = 16
SLOTS = 5
SIDE = 256
BLOCK = 128


_STAGED = {}
_LOADED = {}


def push_rhs(w, staging_register, mxu_index):
    _STAGED[(mxu_index, staging_register)] = w


def acc_lhs(acc, lhs, load_staged_rhs, q):
    if load_staged_rhs is not None:
        _LOADED[q] = _STAGED[(q, load_staged_rhs)]
    acc[...] += jnp.dot(lhs, _LOADED[q], preferred_element_type=jnp.float32)


def pop(acc):
    v = acc[...]
    acc[...] = jnp.zeros_like(v)
    return v


def _kernel(n_sp, repeats, cycle, rows, x_ref, wp_ref, wn_ref, b_ref, wr_ref, ws_ref,
            skip, h_ref, hb, ps, g_s, wpb, wnb, wrb, wsb, wsem, xsem, osem, send_sem, recv_sem):
    me = lax.axis_index("sp")
    layers = repeats * cycle
    ch = x_ref.shape[1]
    gate = wn_ref.shape[2] // 2
    nb = rows // BLOCK
    pads = [max(TILE, 2 ** k) for k in range(cycle)]
    stack_rows = sum(pads) + cycle * rows

    def base_of(s, k):
        return s * stack_rows + sum(pads[:k]) + k * rows

    def local_of(s, k):
        return base_of(s, k) + pads[k % cycle]

    def weight_copies(layer, slot):
        pairs = ((wp_ref, wpb), (wn_ref, wnb), (wr_ref, wrb), (ws_ref, wsb))
        return [pltpu.make_async_copy(src.at[layer], dst.at[slot], wsem.at[slot, i]) for i, (src, dst) in enumerate(pairs)]

    def halo_copy(s, k):
        base = base_of(s, k)
        return pltpu.make_async_remote_copy(
            src_ref=hb.at[pl.ds(pl.multiple_of(base + rows, TILE), pads[k]), :],
            dst_ref=hb.at[pl.ds(pl.multiple_of(base, TILE), pads[k]), :],
            send_sem=send_sem.at[s, k], recv_sem=recv_sem.at[s, k],
            device_id={"sp": jnp.minimum(me + 1, n_sp - 1)}, device_id_type=pl.DeviceIdType.MESH)

    def at(start, size):
        return pl.ds(pl.multiple_of(start, TILE), size)

    def body(acc0, acc1):
        X = (acc0[:nb], acc1[:nb])
        Y = (acc0[nb:], acc1[nb:])

        def steps_of(s, k):
            slot = k % SLOTS
            local = local_of(s, k)
            d = 2 ** (k % cycle)

            def here(kt):
                return lambda q, i: hb[at(local + i * BLOCK, BLOCK), kt * SIDE:(kt + 1) * SIDE]

            def past(kt):
                if d < TILE:
                    return lambda q, i: ps[i * BLOCK:(i + 1) * BLOCK, kt * SIDE:(kt + 1) * SIDE]
                return lambda q, i: hb[at(local - d + i * BLOCK, BLOCK), kt * SIDE:(kt + 1) * SIDE]

            def gated(kt):
                return lambda q, i: g_s[i * BLOCK:(i + 1) * BLOCK, kt * SIDE:(kt + 1) * SIDE]

            def gated_half(kt):
                return lambda q, i: g_s[q * (rows // 2) + i * BLOCK:q * (rows // 2) + (i + 1) * BLOCK, kt * SIDE:(kt + 1) * SIDE]

            def w(buf, kt, col):
                return lambda q: buf[slot, kt * SIDE:(kt + 1) * SIDE, col(q):col(q) + SIDE]

            out = []
            for acc, j in ((X, 0), (Y, 1)):
                out += [(w(wnb, kt, lambda q, j=j: q * gate + j * SIDE), here(kt), acc, nb) for kt in range(2)]
            for acc, j in ((X, 0), (Y, 1)):
                out += [(w(wpb, kt, lambda q, j=j: q * gate + j * SIDE), past(kt), acc, nb) for kt in range(2)]
            out += [(w(wrb, kt, lambda q: q * SIDE), gated(kt), X, nb) for kt in range(2)]
            out += [(w(wsb, kt, lambda q: 0), gated_half(kt), Y, nb // 2) for kt in range(2)]
            return out

        def push(step, n):
            for q in range(2):
                push_rhs(step[0](q), staging_register=n % 2, mxu_index=q)

        def run(step, following, n):
            for i in range(step[3]):
                for q in range(2):
                    acc_lhs(step[2][q][i], step[1](q, i), n % 2 if i == 0 else None, q)
                if i == 0:
                    push(following, n + 1)

        def gate_half(s, k, acc, j):
            ba = b_ref[k, pl.ds(s, 1), j * SIDE:(j + 1) * SIDE]
            bt = b_ref[k, pl.ds(s, 1), gate + j * SIDE:gate + (j + 1) * SIDE]
            for i in range(nb):
                a = jnp.tanh(pop(acc[0][i]) + ba)
                t = jnp.tanh(0.5 * (pop(acc[1][i]) + bt))
                g_s[i * BLOCK:(i + 1) * BLOCK, j * SIDE:(j + 1) * SIDE] = (a * (0.5 * t + 0.5)).astype(jnp.bfloat16)

        def take_skip():
            for q in range(2):
                for i in range(nb // 2):
                    lo = q * (rows // 2) + i * BLOCK
                    skip[lo:lo + BLOCK, :] += pop(Y[q][i])

        def take_res(s, k):
            old, new = local_of(s, k), local_of(s, k + 1)
            for i in range(nb):
                for q in range(2):
                    cols = slice(q * SIDE, (q + 1) * SIDE)
                    v = hb[at(old + i * BLOCK, BLOCK), cols].astype(jnp.float32) + pop(X[q][i])
                    hb[at(new + i * BLOCK, BLOCK), cols] = v.astype(hb.dtype)

        for q in range(2):
            for i in range(nb):
                X[q][i][...] = jnp.zeros_like(X[q][i])
                Y[q][i][...] = jnp.zeros_like(Y[q][i])
        for c in weight_copies(0, 0):
            c.wait()
        x_copy.wait()
        first = steps_of(0, 0)
        push(first[0], 0)
        run(first[0], first[1], 0)

        def stack(s, carry):
            push(steps_of(s, 0)[1], 1)
            for k in range(cycle):
                layer = s * cycle + k
                st = steps_of(s, k)
                nxt = steps_of(s, k + 1)
                d = 2 ** k

                @pl.when(me < n_sp - 1)
                def _():
                    halo_copy(s, k).start()

                def fetch():
                    for c in weight_copies(layer + SLOTS - 1, (k + SLOTS - 1) % SLOTS):
                        c.start()

                def arrive():
                    for c in weight_copies(layer + 1, (k + 1) % SLOTS):
                        c.wait()
                if k + SLOTS - 1 < cycle:
                    fetch()
                else:
                    pl.when(s < repeats - 1)(fetch)
                if k + 1 < cycle:
                    arrive()
                else:
                    pl.when(s < repeats - 1)(arrive)
                take_skip()
                run(st[1], st[2], 1)
                local = local_of(s, k)
                if d < TILE:
                    ps[TILE:rows, :] = hb[at(local, rows), :][TILE - d:rows - d, :]
                run(st[2], st[3], 2)
                run(st[3], st[4], 3)

                @pl.when(me > 0)
                def _():
                    halo_copy(s, k).wait_recv()
                if d < TILE:
                    ps[0:TILE, :] = hb[at(local - TILE, 2 * TILE), :][TILE - d:2 * TILE - d, :]
                run(st[4], st[5], 4)
                run(st[5], st[6], 5)
                gate_half(s, k, X, 0)
                run(st[6], st[7], 6)
                run(st[7], st[8], 7)
                gate_half(s, k, Y, 1)
                run(st[8], st[9], 8)
                run(st[9], st[10], 9)
                run(st[10], st[11], 10)
                run(st[11], nxt[0], 11)
                take_res(s, k)
                run(nxt[0], nxt[1], 12)
            return carry

        lax.fori_loop(0, repeats, stack, 0)
        take_skip()
        for q in range(2):
            pass
            for i in range(nb):
                pop(X[q][i])

    x_copy = pltpu.make_async_copy(x_ref, hb.at[pl.ds(pads[0], rows), :], xsem)
    x_copy.start()
    for slot in range(SLOTS - 1):
        for c in weight_copies(slot, slot):
            c.start()
    barrier = pltpu.get_barrier_semaphore()

    @pl.when(me > 0)
    def _():
        pl.semaphore_signal(barrier, inc=1, device_id={"sp": me - 1}, device_id_type=pl.DeviceIdType.MESH)

    @pl.when(me == 0)
    def _():
        for s in range(repeats):
            for k in range(cycle):
                hb[base_of(s, k):base_of(s, k) + pads[k], :] = jnp.zeros((pads[k], ch), hb.dtype)

    skip[...] = jnp.zeros_like(skip)

    @pl.when(me < n_sp - 1)
    def _():
        pl.semaphore_wait(barrier, 1)

    specs = tuple(pltpu.VMEM((BLOCK, SIDE), jnp.float32) for q in range(2) for _ in range(2 * nb))
    pl.run_scoped(lambda *refs: body(refs[:2 * nb], refs[2 * nb:]), *specs)

    out_copy = pltpu.make_async_copy(hb.at[pl.ds(local_of(repeats - 1, cycle), rows), :], h_ref, osem)
    out_copy.start()
    out_copy.wait()

    @pl.when(me < n_sp - 1)
    def _():
        for s in range(repeats):
            for k in range(cycle):
                halo_copy(s, k).wait_send()


def _head(skip, h_ref, w1_ref, c1_ref, w2_ref, c2_ref, y_ref, out_ref):
    out_ref[...] = h_ref[...]
    act = jnp.maximum(skip[...], 0.0).astype(jnp.bfloat16)
    mid = jnp.dot(act, w1_ref[...], preferred_element_type=jnp.float32) + c1_ref[...]
    mid = jnp.maximum(mid, 0.0).astype(jnp.bfloat16)
    y_ref[...] = jnp.dot(mid, w2_ref[...], preferred_element_type=jnp.float32) + c2_ref[...]


def solution(mesh):
    n_sp = mesh.shape["sp"]
    row_spec = P(("ens", "sp"), None)

    def local_stack(x_seq, w_past, w_now, b_conv, w_res, w_skip, w_out1, b_out1, w_out2, b_out2):
        repeats, cycle, ch, wide = w_past.shape
        layers, rows = repeats * cycle, x_seq.shape[0]
        gate, skips = w_res.shape[2], w_skip.shape[3]
        classes = w_out2.shape[1]
        pads = [max(TILE, 2 ** k) for k in range(cycle)]
        region = repeats * (sum(pads) + cycle * rows) + pads[0] + rows
        hbm = pl.BlockSpec(memory_space=pltpu.HBM)
        vmem = pl.BlockSpec(memory_space=pltpu.VMEM)
        anywhere = pl.BlockSpec(memory_space=pl.ANY)
        skip, h = pl.pallas_call(
            functools.partial(_kernel, n_sp, repeats, cycle, rows),
            name="stack",
            out_shape=(jax.ShapeDtypeStruct((rows, skips), jnp.float32), jax.ShapeDtypeStruct((rows, ch), x_seq.dtype)),
            in_specs=[hbm, hbm, hbm, vmem, hbm, hbm],
            out_specs=(vmem, anywhere),
            scratch_shapes=[
                pltpu.VMEM((region, ch), x_seq.dtype),
                pltpu.VMEM((rows, ch), x_seq.dtype),
                pltpu.VMEM((rows, gate), jnp.bfloat16),
                pltpu.VMEM((SLOTS, ch, wide), w_past.dtype),
                pltpu.VMEM((SLOTS, ch, wide), w_now.dtype),
                pltpu.VMEM((SLOTS, gate, ch), w_res.dtype),
                pltpu.VMEM((SLOTS, gate, skips), w_skip.dtype),
                pltpu.SemaphoreType.DMA((SLOTS, 4)),
                pltpu.SemaphoreType.DMA,
                pltpu.SemaphoreType.DMA,
                pltpu.SemaphoreType.DMA((repeats, cycle)),
                pltpu.SemaphoreType.DMA((repeats, cycle)),
            ],
            compiler_params=pltpu.CompilerParams(collective_id=0, has_side_effects=True, vmem_limit_bytes=46 * 2 ** 20),
        )(x_seq, w_past.reshape(layers, ch, wide), w_now.reshape(layers, ch, wide), jnp.transpose(b_conv, (1, 0, 2)),
          w_res.reshape(layers, gate, ch), w_skip.reshape(layers, gate, skips))
        return pl.pallas_call(
            _head,
            name="head",
            out_shape=(jax.ShapeDtypeStruct((rows, classes), jnp.float32), jax.ShapeDtypeStruct((rows, ch), x_seq.dtype)),
            in_specs=[vmem] * 6,
            out_specs=(vmem, vmem),
        )(skip, h, w_out1, b_out1.reshape(1, -1), w_out2, b_out2.reshape(1, -1))

    return jax.shard_map(
        local_stack,
        mesh=mesh,
        in_specs=(row_spec, P(), P(), P(), P(), P(), P(), P(), P(), P()),
        out_specs=(row_spec, row_spec),
        check_vma=False,
    )
```

time: 80.5 us -> 77.6 us (0.964)
  local copies, waits for them, and re-layouts: 5.4 us -> 3.54 us
  Pallas kernels: 74.3 us -> 73.2 us
    pallas_call x1, Pallas kernels: 74.3 us -> 70.6 us  [local_stack(): pl.pallas_call(functools.partial(_kernel, n_sp, repeats, cycle, rows), na...]
    pallas_call x0 -> x1, Pallas kernels: none -> 2.6 us  [local_stack(): pl.pallas_call(_head, name='head', out_shape=(jax.ShapeDtypeStruct((rows,...]
    unnamed x3 -> x8, local copies, waits for them, and re-layouts: 4.73 us -> 3.54 us
where the time goes in v1:
time: 77.6 us; the launch traced here: 77.4 us
  Pallas kernels  73.2 us (94%)
  local copies, waits for them, and re-layouts  3.54 us (5%)
    pallas_call x1, Pallas kernels, local_stack(): pl.pallas_call(functools.partial(_kernel, n_sp, repeats, cycle, rows), na...  70.6 us
    unnamed x8, local copies, waits for them, and re-layouts  3.54 us
    pallas_call x1, Pallas kernels, local_stack(): pl.pallas_call(_head, name='head', out_shape=(jax.ShapeDtypeStruct((rows,...  2.6 us

profile of v1, /device:TPU:7, one launch (start us, length us, event | category | flops | bytes accessed | tf_op | source)
XLA Modules:
  0.0 77.4 jit_solution(12631498161640940872)
XLA Ops:
  0.6 0.0 copy-start
  0.6 1.0 %copy-done = bf16[512,512]{1,0:T(8,128)(2,1)S(1)} copy-done((bf16[512,512]{1,0:T(8,128)(2,1)S(1)}, bf16[512,512]{1,0:T(8,128)(2,1)}, u32[]{:S(2)}) %copy-start) | copy-done | bytes 524312
  1.7 0.0 copy-start.3
  1.7 0.9 %copy-done.3 = f32[3,10,1024]{2,0,1:T(4,128)S(1)} copy-done((f32[3,10,1024]{2,0,1:T(4,128)S(1)}, f32[3,10,1024]{2,0,1:T(4,128)}, u32[]{:S(2)}) %copy-start.3) | copy-done | bytes 122904
  2.6 70.6 %stack.1 = (f32[512,256]{1,0:T(8,128)S(1)}, bf16[512,512]{1,0:T(8,128)(2,1)S(1)}) custom-call(bf16[512,512]{1,0:T(8,128)(2,1)S(1)} %copy-done, bf16[30,512,1024]{2,1,0:T(8,128)(2,1)} %bitcast.8, bf16[30,512,1024]{2,1,0:T(8,128)(2,1)} %bitcast.9, f32[10,3,1024]{2,1,0:T(4,128)S(1)} %bitcast.7, bf16[30,512,512]{2,1,0:T(8,128)(2,1)} %bitcast.10, ...), custom_call_target="tpu_custom_call" | custom-call | tf_op jit(solution)/shard_map/stack/pallas_call | solution.py:266
  73.2 0.0 copy-start.1
  73.2 0.8 %copy-done.1 = f32[512,256]{1,0:T(8,128)} copy-done((f32[512,256]{1,0:T(8,128)}, f32[512,256]{1,0:T(8,128)S(1)}, u32[]{:S(2)}) %copy-start.1) | copy-done | bytes 524312
  74.0 0.0 copy-start.2
  74.0 0.8 %copy-done.2 = bf16[512,512]{1,0:T(8,128)(2,1)} copy-done((bf16[512,512]{1,0:T(8,128)(2,1)}, bf16[512,512]{1,0:T(8,128)(2,1)S(1)}, u32[]{:S(2)}) %copy-start.2) | copy-done | bytes 524312
  74.8 2.6 %head.1 = (f32[512,256]{1,0:T(8,128)}, bf16[512,512]{1,0:T(8,128)(2,1)}) custom-call(f32[512,256]{1,0:T(8,128)} %copy-done.1, bf16[512,512]{1,0:T(8,128)(2,1)} %copy-done.2, bf16[256,256]{1,0:T(8,128)(2,1)} %w1_ref.1, f32[1,256]{1,0:T(1,128)} %bitcast.12, bf16[256,256]{1,0:T(8,128)(2,1)} %w2_ref.1, f32[1,256]{1,0:T(1,128)} %bitcast.13), custom_call_target="tpu_custom_call" | custom-call | tf_op jit(solution)/shard_map/head/pallas_call | solution.py:289
Async XLA Ops:
  0.6 1.0 %copy-start = (bf16[512,512]{1,0:T(8,128)(2,1)S(1)}, bf16[512,512]{1,0:T(8,128)(2,1)}, u32[]{:S(2)}) copy-start(bf16[512,512]{1,0:T(8,128)(2,1)} %x_ref.1) | copy-start | bytes 1572868
  1.7 0.9 %copy-start.3 = (f32[3,10,1024]{2,0,1:T(4,128)S(1)}, f32[3,10,1024]{2,0,1:T(4,128)}, u32[]{:S(2)}) copy-start(f32[3,10,1024]{2,0,1:T(4,128)} %param.13) | copy-start | bytes 368644
  73.2 0.8 %copy-start.1 = (f32[512,256]{1,0:T(8,128)}, f32[512,256]{1,0:T(8,128)S(1)}, u32[]{:S(2)}) copy-start(f32[512,256]{1,0:T(8,128)S(1)} %get-tuple-element.4.skip) | copy-start | bytes 1572868
  74.0 0.8 %copy-start.2 = (bf16[512,512]{1,0:T(8,128)(2,1)}, bf16[512,512]{1,0:T(8,128)(2,1)S(1)}, u32[]{:S(2)}) copy-start(bf16[512,512]{1,0:T(8,128)(2,1)S(1)} %get-tuple-element.5.h_ref) | copy-start | bytes 1572868

commit v2 on v0

v2 whole, which is shorter than its diff:
```python
import functools

import jax
import jax.numpy as jnp
from jax import lax
from jax.experimental import pallas as pl
from jax.experimental.pallas import tpu as pltpu
from jax.sharding import PartitionSpec as P

TILE = 16
SLOTS = 5
SIDE = 256
BLOCK = 128


def _kernel(n_sp, repeats, cycle, rows, x_ref, wp_ref, wn_ref, b_ref, wr_ref, ws_ref,
            skip, h_ref, hb, ps, g_s, wpb, wnb, wrb, wsb, wsem, xsem, osem, send_sem, recv_sem):
    me = lax.axis_index("sp")
    layers = repeats * cycle
    ch = x_ref.shape[1]
    gate = wn_ref.shape[2] // 2
    nb = rows // BLOCK
    pads = [max(TILE, 2 ** k) for k in range(cycle)]
    stack_rows = sum(pads) + cycle * rows

    def base_of(s, k):
        return s * stack_rows + sum(pads[:k]) + k * rows

    def local_of(s, k):
        return base_of(s, k) + pads[k % cycle]

    def weight_copies(layer, slot):
        pairs = ((wp_ref, wpb), (wn_ref, wnb), (wr_ref, wrb), (ws_ref, wsb))
        return [pltpu.make_async_copy(src.at[layer], dst.at[slot], wsem.at[slot, i]) for i, (src, dst) in enumerate(pairs)]

    def halo_copy(s, k):
        base = base_of(s, k)
        return pltpu.make_async_remote_copy(
            src_ref=hb.at[pl.ds(pl.multiple_of(base + rows, TILE), pads[k]), :],
            dst_ref=hb.at[pl.ds(pl.multiple_of(base, TILE), pads[k]), :],
            send_sem=send_sem.at[s, k], recv_sem=recv_sem.at[s, k],
            device_id={"sp": jnp.minimum(me + 1, n_sp - 1)}, device_id_type=pl.DeviceIdType.MESH)

    def at(start, size):
        return pl.ds(pl.multiple_of(start, TILE), size)

    def stack(s, carry):
        for k in range(cycle):
            layer, slot, d = s * cycle + k, k % SLOTS, 2 ** k
            local, new = local_of(s, k), local_of(s, k + 1)

            @pl.when(me < n_sp - 1)
            def _():
                halo_copy(s, k).start()

            def fetch():
                for c in weight_copies(layer + SLOTS - 1, (k + SLOTS - 1) % SLOTS):
                    c.start()
            if k + SLOTS - 1 < cycle:
                fetch()
            else:
                pl.when(s < repeats - 1)(fetch)
            for c in weight_copies(layer, slot):
                c.wait()

            @pl.when(me > 0)
            def _():
                halo_copy(s, k).wait_recv()
            here = hb[at(local, rows), :]
            if d < TILE:
                past = hb[at(local - TILE, rows + TILE), :][TILE - d:TILE - d + rows, :]
            else:
                past = hb[at(local - d, rows), :]
            for j in range(gate // SIDE):
                ca, ct = j * SIDE, gate + j * SIDE

                def both(buf):
                    return jnp.concatenate([buf[slot, :, ca:ca + SIDE], buf[slot, :, ct:ct + SIDE]], axis=1)
                z = (jnp.dot(past, both(wpb), preferred_element_type=jnp.float32)
                     + jnp.dot(here, both(wnb), preferred_element_type=jnp.float32))
                a = jnp.tanh(z[:, :SIDE] + b_ref[k, pl.ds(s, 1), ca:ca + SIDE])
                t = jnp.tanh(0.5 * (z[:, SIDE:] + b_ref[k, pl.ds(s, 1), ct:ct + SIDE]))
                g_s[:, ca:ca + SIDE] = (a * (0.5 * t + 0.5)).astype(jnp.bfloat16)
            g = g_s[...]
            res = here.astype(jnp.float32) + jnp.dot(g, wrb[slot], preferred_element_type=jnp.float32)
            hb[at(new, rows), :] = res.astype(hb.dtype)
            half = rows // 2
            for q in range(2):
                skip[q * half:(q + 1) * half, :] += jnp.dot(g[q * half:(q + 1) * half, :], wsb[slot], preferred_element_type=jnp.float32)
        return carry

    x_copy = pltpu.make_async_copy(x_ref, hb.at[pl.ds(pads[0], rows), :], xsem)
    x_copy.start()
    for slot in range(SLOTS - 1):
        for c in weight_copies(slot, slot):
            c.start()
    barrier = pltpu.get_barrier_semaphore()

    @pl.when(me > 0)
    def _():
        pl.semaphore_signal(barrier, inc=1, device_id={"sp": me - 1}, device_id_type=pl.DeviceIdType.MESH)

    @pl.when(me == 0)
    def _():
        for s in range(repeats):
            for k in range(cycle):
                hb[base_of(s, k):base_of(s, k) + pads[k], :] = jnp.zeros((pads[k], ch), hb.dtype)

    skip[...] = jnp.zeros_like(skip)

    @pl.when(me < n_sp - 1)
    def _():
        pl.semaphore_wait(barrier, 1)

    x_copy.wait()
    lax.fori_loop(0, repeats, stack, 0)

    out_copy = pltpu.make_async_copy(hb.at[pl.ds(local_of(repeats - 1, cycle), rows), :], h_ref, osem)
    out_copy.start()
    out_copy.wait()

    @pl.when(me < n_sp - 1)
    def _():
        for s in range(repeats):
            for k in range(cycle):
                halo_copy(s, k).wait_send()


def _head(skip, h_ref, w1_ref, c1_ref, w2_ref, c2_ref, y_ref, out_ref):
    out_ref[...] = h_ref[...]
    act = jnp.maximum(skip[...], 0.0).astype(jnp.bfloat16)
    mid = jnp.dot(act, w1_ref[...], preferred_element_type=jnp.float32) + c1_ref[...]
    mid = jnp.maximum(mid, 0.0).astype(jnp.bfloat16)
    y_ref[...] = jnp.dot(mid, w2_ref[...], preferred_element_type=jnp.float32) + c2_ref[...]


def solution(mesh):
    n_sp = mesh.shape["sp"]
    row_spec = P(("ens", "sp"), None)

    def local_stack(x_seq, w_past, w_now, b_conv, w_res, w_skip, w_out1, b_out1, w_out2, b_out2):
        repeats, cycle, ch, wide = w_past.shape
        layers, rows = repeats * cycle, x_seq.shape[0]
        gate, skips = w_res.shape[2], w_skip.shape[3]
        classes = w_out2.shape[1]
        pads = [max(TILE, 2 ** k) for k in range(cycle)]
        region = repeats * (sum(pads) + cycle * rows) + pads[0] + rows
        hbm = pl.BlockSpec(memory_space=pltpu.HBM)
        vmem = pl.BlockSpec(memory_space=pltpu.VMEM)
        anywhere = pl.BlockSpec(memory_space=pl.ANY)
        skip, h = pl.pallas_call(
            functools.partial(_kernel, n_sp, repeats, cycle, rows),
            name="stack",
            out_shape=(jax.ShapeDtypeStruct((rows, skips), jnp.float32), jax.ShapeDtypeStruct((rows, ch), x_seq.dtype)),
            in_specs=[hbm, hbm, hbm, vmem, hbm, hbm],
            out_specs=(vmem, anywhere),
            scratch_shapes=[
                pltpu.VMEM((region, ch), x_seq.dtype),
                pltpu.VMEM((rows, ch), x_seq.dtype),
                pltpu.VMEM((rows, gate), jnp.bfloat16),
                pltpu.VMEM((SLOTS, ch, wide), w_past.dtype),
                pltpu.VMEM((SLOTS, ch, wide), w_now.dtype),
                pltpu.VMEM((SLOTS, gate, ch), w_res.dtype),
                pltpu.VMEM((SLOTS, gate, skips), w_skip.dtype),
                pltpu.SemaphoreType.DMA((SLOTS, 4)),
                pltpu.SemaphoreType.DMA,
                pltpu.SemaphoreType.DMA,
                pltpu.SemaphoreType.DMA((repeats, cycle)),
                pltpu.SemaphoreType.DMA((repeats, cycle)),
            ],
            compiler_params=pltpu.CompilerParams(collective_id=0, has_side_effects=True, vmem_limit_bytes=46 * 2 ** 20),
        )(x_seq, w_past.reshape(layers, ch, wide), w_now.reshape(layers, ch, wide), jnp.transpose(b_conv, (1, 0, 2)),
          w_res.reshape(layers, gate, ch), w_skip.reshape(layers, gate, skips))
        return pl.pallas_call(
            _head,
            name="head",
            out_shape=(jax.ShapeDtypeStruct((rows, classes), jnp.float32), jax.ShapeDtypeStruct((rows, ch), x_seq.dtype)),
            in_specs=[vmem] * 6,
            out_specs=(vmem, vmem),
        )(skip, h, w_out1, b_out1.reshape(1, -1), w_out2, b_out2.reshape(1, -1))

    return jax.shard_map(
        local_stack,
        mesh=mesh,
        in_specs=(row_spec, P(), P(), P(), P(), P(), P(), P(), P(), P()),
        out_specs=(row_spec, row_spec),
        check_vma=False,
    )
```

time: 80.5 us -> 68.7 us (0.85)
  Pallas kernels: 74.3 us -> 64.4 us
  local copies, waits for them, and re-layouts: 5.4 us -> 3.54 us
    pallas_call x1, Pallas kernels: 74.3 us -> 61.8 us  [local_stack(): pl.pallas_call(functools.partial(_kernel, n_sp, repeats, cycle, rows), na...]
    pallas_call x0 -> x1, Pallas kernels: none -> 2.6 us  [local_stack(): pl.pallas_call(_head, name='head', out_shape=(jax.ShapeDtypeStruct((rows,...]
    unnamed x3 -> x8, local copies, waits for them, and re-layouts: 4.73 us -> 3.54 us
where the time goes in v2:
time: 68.7 us; the launch traced here: 68.6 us
  Pallas kernels  64.4 us (94%)
  local copies, waits for them, and re-layouts  3.54 us (5%)
    pallas_call x1, Pallas kernels, local_stack(): pl.pallas_call(functools.partial(_kernel, n_sp, repeats, cycle, rows), na...  61.8 us
    unnamed x8, local copies, waits for them, and re-layouts  3.54 us
    pallas_call x1, Pallas kernels, local_stack(): pl.pallas_call(_head, name='head', out_shape=(jax.ShapeDtypeStruct((rows,...  2.6 us

profile of v2, /device:TPU:7, one launch (start us, length us, event | category | flops | bytes accessed | tf_op | source)
XLA Modules:
  0.0 68.6 jit_solution(11462434441360262729)
XLA Ops:
  0.6 0.0 copy-start
  0.6 1.0 %copy-done = bf16[512,512]{1,0:T(8,128)(2,1)S(1)} copy-done((bf16[512,512]{1,0:T(8,128)(2,1)S(1)}, bf16[512,512]{1,0:T(8,128)(2,1)}, u32[]{:S(2)}) %copy-start) | copy-done | bytes 524312
  1.7 0.0 copy-start.3
  1.7 0.9 %copy-done.3 = f32[3,10,1024]{2,0,1:T(4,128)S(1)} copy-done((f32[3,10,1024]{2,0,1:T(4,128)S(1)}, f32[3,10,1024]{2,0,1:T(4,128)}, u32[]{:S(2)}) %copy-start.3) | copy-done | bytes 122904
  2.6 61.8 %stack.1 = (f32[512,256]{1,0:T(8,128)S(1)}, bf16[512,512]{1,0:T(8,128)(2,1)S(1)}) custom-call(bf16[512,512]{1,0:T(8,128)(2,1)S(1)} %copy-done, bf16[30,512,1024]{2,1,0:T(8,128)(2,1)} %bitcast.8, bf16[30,512,1024]{2,1,0:T(8,128)(2,1)} %bitcast.9, f32[10,3,1024]{2,1,0:T(4,128)S(1)} %bitcast.7, bf16[30,512,512]{2,1,0:T(8,128)(2,1)} %bitcast.10, ...), custom_call_target="tpu_custom_call" | custom-call | tf_op jit(solution)/shard_map/stack/pallas_call | solution.py:151
  64.4 0.0 copy-start.1
  64.4 0.8 %copy-done.1 = f32[512,256]{1,0:T(8,128)} copy-done((f32[512,256]{1,0:T(8,128)}, f32[512,256]{1,0:T(8,128)S(1)}, u32[]{:S(2)}) %copy-start.1) | copy-done | bytes 524312
  65.2 0.0 copy-start.2
  65.2 0.8 %copy-done.2 = bf16[512,512]{1,0:T(8,128)(2,1)} copy-done((bf16[512,512]{1,0:T(8,128)(2,1)}, bf16[512,512]{1,0:T(8,128)(2,1)S(1)}, u32[]{:S(2)}) %copy-start.2) | copy-done | bytes 524312
  66.0 2.6 %head.1 = (f32[512,256]{1,0:T(8,128)}, bf16[512,512]{1,0:T(8,128)(2,1)}) custom-call(f32[512,256]{1,0:T(8,128)} %copy-done.1, bf16[512,512]{1,0:T(8,128)(2,1)} %copy-done.2, bf16[256,256]{1,0:T(8,128)(2,1)} %w1_ref.1, f32[1,256]{1,0:T(1,128)} %bitcast.12, bf16[256,256]{1,0:T(8,128)(2,1)} %w2_ref.1, f32[1,256]{1,0:T(1,128)} %bitcast.13), custom_call_target="tpu_custom_call" | custom-call | tf_op jit(solution)/shard_map/head/pallas_call | solution.py:174
Async XLA Ops:
  0.6 1.0 %copy-start = (bf16[512,512]{1,0:T(8,128)(2,1)S(1)}, bf16[512,512]{1,0:T(8,128)(2,1)}, u32[]{:S(2)}) copy-start(bf16[512,512]{1,0:T(8,128)(2,1)} %x_ref.1) | copy-start | bytes 1572868
  1.7 0.9 %copy-start.3 = (f32[3,10,1024]{2,0,1:T(4,128)S(1)}, f32[3,10,1024]{2,0,1:T(4,128)}, u32[]{:S(2)}) copy-start(f32[3,10,1024]{2,0,1:T(4,128)} %param.13) | copy-start | bytes 368644
  64.4 0.8 %copy-start.1 = (f32[512,256]{1,0:T(8,128)}, f32[512,256]{1,0:T(8,128)S(1)}, u32[]{:S(2)}) copy-start(f32[512,256]{1,0:T(8,128)S(1)} %get-tuple-element.4.skip) | copy-start | bytes 1572868
  65.2 0.8 %copy-start.2 = (bf16[512,512]{1,0:T(8,128)(2,1)}, bf16[512,512]{1,0:T(8,128)(2,1)S(1)}, u32[]{:S(2)}) copy-start(bf16[512,512]{1,0:T(8,128)(2,1)S(1)} %get-tuple-element.5.h_ref) | copy-start | bytes 1572868

commit v3 on v2

v3 whole, which is shorter than its diff:
```python
import functools

import jax
import jax.numpy as jnp
from jax import lax
from jax.experimental import pallas as pl
from jax.experimental.pallas import tpu as pltpu
from jax.sharding import PartitionSpec as P

TILE = 16
SLOTS = 5
SIDE = 256
SPLIT = (0, 1, 2, 3, 4, 5, 6, 7, 8, 9)
EARLY = 0


def _kernel(n_sp, repeats, cycle, rows, x_ref, wp_ref, wn_ref, b_ref, wr_ref, ws_ref,
            skip, h_ref, *scratch):
    hb, (g_s, b_s, wpb, wnb, wrb, wsb, wsem, xsem, bsem, send_sem, recv_sem) = scratch[:cycle], scratch[cycle:]
    me = lax.axis_index("sp")
    layers = repeats * cycle
    ch = x_ref.shape[1]
    gate = wn_ref.shape[2] // 2
    half = rows // 2
    pads = [max(TILE, 2 ** k) for k in range(cycle)]

    def weight_copies(layer, slot):
        pairs = ((wn_ref, wnb), (wp_ref, wpb), (wr_ref, wrb), (ws_ref, wsb))
        return [pltpu.make_async_copy(src.at[layer], dst.at[slot], wsem.at[slot, i]) for i, (src, dst) in enumerate(pairs)]

    def halo_copies(s, k):
        parts = [(pads[k] - half, half), (0, half)] if pads[k] > half else [(0, pads[k])]
        return [pltpu.make_async_remote_copy(
            src_ref=hb[k].at[s, rows + lo:rows + lo + n, :], dst_ref=hb[k].at[s, lo:lo + n, :],
            send_sem=send_sem.at[s, k, i], recv_sem=recv_sem.at[s, k, i],
            device_id={"sp": jnp.minimum(me + 1, n_sp - 1)}, device_id_type=pl.DeviceIdType.MESH) for i, (lo, n) in enumerate(parts)]

    def stack(s, carry):
        for k in range(cycle):
            layer, slot, d = s * cycle + k, k % SLOTS, 2 ** k
            after = (s, k + 1) if k + 1 < cycle else (s + 1, 0)
            old, new = hb[k].at[s], hb[after[1]].at[after[0]]
            pad, new_pad = pads[k], pads[after[1]]

            def send(part):
                ok = me < n_sp - 1
                if k + 1 == cycle:
                    ok &= s < repeats - 1
                pl.when(ok)(lambda: halo_copies(*after)[part].start())

            def receive(part):
                pl.when(me > 0)(lambda: halo_copies(s, k)[part].wait_recv())

            def fetch():
                for c in weight_copies(layer + SLOTS - 1, (k + SLOTS - 1) % SLOTS):
                    c.start()
            if k + SLOTS - 1 < cycle:
                fetch()
            else:
                pl.when(s < repeats - 1)(fetch)
            for c in weight_copies(layer, slot):
                c.wait()

            def both(buf, j):
                ca, ct = j * SIDE, gate + j * SIDE
                return jnp.concatenate([buf[slot, :, ca:ca + SIDE], buf[slot, :, ct:ct + SIDE]], axis=1)

            def now(lo, n, j):
                return jnp.dot(old[pad + lo:pad + lo + n, :], both(wnb, j), preferred_element_type=jnp.float32)

            def past(lo, n, j):
                if d < TILE:
                    rows_in = old[pad + lo - TILE:pad + lo + n, :][TILE - d:TILE - d + n, :]
                else:
                    rows_in = old[pad + lo - d:pad + lo - d + n, :]
                return jnp.dot(rows_in, both(wpb, j), preferred_element_type=jnp.float32)

            def gated(lo, n, j, z):
                ca, ct = j * SIDE, gate + j * SIDE
                a = jnp.tanh(z[:, :SIDE] + b_s[k, pl.ds(s, 1), ca:ca + SIDE])
                t = jnp.tanh(0.5 * (z[:, SIDE:] + b_s[k, pl.ds(s, 1), ct:ct + SIDE]))
                g_s[lo:lo + n, ca:ca + SIDE] = (a * (0.5 * t + 0.5)).astype(jnp.bfloat16)

            def residual(lo, n):
                res = jnp.dot(g_s[lo:lo + n, :], wrb[slot], preferred_element_type=jnp.float32)
                new[new_pad + lo:new_pad + lo + n, :] = (old[pad + lo:pad + lo + n, :].astype(jnp.float32) + res).astype(new.dtype)

            if k in SPLIT:
                zn = [now(half, half, j) for j in range(2)]
                if d > half:
                    receive(0)
                for j in range(2):
                    gated(half, half, j, past(half, half, j) + zn[j])
                residual(half, half)
                zn = [now(0, half, j) for j in range(2)]
                send(0)
                receive(1 if d > half else 0)
                for j in range(2):
                    gated(0, half, j, past(0, half, j) + zn[j])
                residual(0, half)
                for lo in (half, 0):
                    skip[lo:lo + half, :] += jnp.dot(g_s[lo:lo + half, :], wsb[slot], preferred_element_type=jnp.float32)
                if new_pad > half:
                    send(1)
            else:
                zn = [now(0, rows, j) for j in range(EARLY if k == cycle - 1 else 0)]
                for i in range(2 if d > half else 1):
                    receive(i)
                for j in range(2):
                    gated(0, rows, j, past(0, rows, j) + (zn[j] if j < len(zn) else now(0, rows, j)))
                residual(0, rows)
                for lo in (half, 0):
                    skip[lo:lo + half, :] += jnp.dot(g_s[lo:lo + half, :], wsb[slot], preferred_element_type=jnp.float32)
                for i in range(2 if new_pad > half else 1):
                    send(i)
        return carry

    x_copy = pltpu.make_async_copy(x_ref, hb[0].at[0, pads[0]:pads[0] + rows, :], xsem)
    b_copy = pltpu.make_async_copy(b_ref, b_s, bsem)
    x_copy.start()
    first = weight_copies(0, 0)
    for c in first:
        c.start()
    b_copy.start()
    barrier = pltpu.get_barrier_semaphore()

    @pl.when(me > 0)
    def _():
        pl.semaphore_signal(barrier, inc=1, device_id={"sp": me - 1}, device_id_type=pl.DeviceIdType.MESH)

    @pl.when(me == 0)
    def _():
        for s in range(repeats):
            for k in range(cycle):
                hb[k][s, 0:pads[k], :] = jnp.zeros((pads[k], ch), hb[k].dtype)

    skip[...] = jnp.zeros_like(skip)
    for layer in range(1, SLOTS - 1):
        for c in weight_copies(layer, layer):
            c.start()
    x_copy.wait()

    @pl.when(me < n_sp - 1)
    def _():
        pl.semaphore_wait(barrier, 1)
        halo_copies(0, 0)[0].start()
    b_copy.wait()
    lax.fori_loop(0, repeats, stack, 0)
    h_ref[...] = hb[0][repeats, pads[0]:pads[0] + rows, :]

    @pl.when(me < n_sp - 1)
    def _():
        for s in range(repeats):
            for k in range(cycle):
                for c in halo_copies(s, k):
                    c.wait_send()


def _head(skip, h_ref, w1_ref, c1_ref, w2_ref, c2_ref, y_ref, out_ref, y_s, ysem, hsem):
    h_copy = pltpu.make_async_copy(h_ref, out_ref, hsem)
    h_copy.start()
    half = y_s.shape[0] // 2
    copies = []
    for i in range(2):
        part = slice(i * half, (i + 1) * half)
        act = jnp.maximum(skip[part, :], 0.0).astype(jnp.bfloat16)
        mid = jnp.dot(act, w1_ref[...], preferred_element_type=jnp.float32) + c1_ref[...]
        mid = jnp.maximum(mid, 0.0).astype(jnp.bfloat16)
        y_s[part, :] = jnp.dot(mid, w2_ref[...], preferred_element_type=jnp.float32) + c2_ref[...]
        copies.append(pltpu.make_async_copy(y_s.at[part, :], y_ref.at[part, :], ysem.at[i]))
        copies[-1].start()
    for c in copies + [h_copy]:
        c.wait()


def solution(mesh):
    n_sp = mesh.shape["sp"]
    row_spec = P(("ens", "sp"), None)

    def local_stack(x_seq, w_past, w_now, b_conv, w_res, w_skip, w_out1, b_out1, w_out2, b_out2):
        repeats, cycle, ch, wide = w_past.shape
        layers, rows = repeats * cycle, x_seq.shape[0]
        gate, skips = w_res.shape[2], w_skip.shape[3]
        classes = w_out2.shape[1]
        pads = [max(TILE, 2 ** k) for k in range(cycle)]
        hbm = pl.BlockSpec(memory_space=pltpu.HBM)
        vmem = pl.BlockSpec(memory_space=pltpu.VMEM)
        skip, h = pl.pallas_call(
            functools.partial(_kernel, n_sp, repeats, cycle, rows),
            name="stack",
            out_shape=(jax.ShapeDtypeStruct((rows, skips), jnp.float32), jax.ShapeDtypeStruct((rows, ch), x_seq.dtype)),
            in_specs=[hbm] * 6,
            out_specs=(vmem, vmem),
            scratch_shapes=[
                *[pltpu.VMEM((repeats + (k == 0), pads[k] + rows, ch), x_seq.dtype) for k in range(cycle)],
                pltpu.VMEM((rows, gate), jnp.bfloat16),
                pltpu.VMEM((cycle, repeats, wide), jnp.float32),
                pltpu.VMEM((SLOTS, ch, wide), w_past.dtype),
                pltpu.VMEM((SLOTS, ch, wide), w_now.dtype),
                pltpu.VMEM((SLOTS, gate, ch), w_res.dtype),
                pltpu.VMEM((SLOTS, gate, skips), w_skip.dtype),
                pltpu.SemaphoreType.DMA((SLOTS, 4)),
                pltpu.SemaphoreType.DMA,
                pltpu.SemaphoreType.DMA,
                pltpu.SemaphoreType.DMA((repeats, cycle, 2)),
                pltpu.SemaphoreType.DMA((repeats, cycle, 2)),
            ],
            compiler_params=pltpu.CompilerParams(collective_id=0, has_side_effects=True, vmem_limit_bytes=46 * 2 ** 20),
        )(pltpu.with_memory_space_constraint(x_seq, pltpu.HBM), w_past.reshape(layers, ch, wide), w_now.reshape(layers, ch, wide), pltpu.with_memory_space_constraint(jnp.transpose(b_conv, (1, 0, 2)), pltpu.HBM),
          w_res.reshape(layers, gate, ch), w_skip.reshape(layers, gate, skips))
        return pl.pallas_call(
            _head,
            name="head",
            out_shape=(jax.ShapeDtypeStruct((rows, classes), jnp.float32), jax.ShapeDtypeStruct((rows, ch), x_seq.dtype)),
            in_specs=[vmem, vmem, vmem, vmem, vmem, vmem],
            out_specs=(hbm, hbm),
            scratch_shapes=[pltpu.VMEM((rows, classes), jnp.float32), pltpu.SemaphoreType.DMA((2,)), pltpu.SemaphoreType.DMA],
            compiler_params=pltpu.CompilerParams(vmem_limit_bytes=8 * 2 ** 20),
        )(skip, h, w_out1, b_out1.reshape(1, -1), w_out2, b_out2.reshape(1, -1))

    return jax.shard_map(
        local_stack,
        mesh=mesh,
        in_specs=(row_spec, P(), P(), P(), P(), P(), P(), P(), P(), P()),
        out_specs=(row_spec, row_spec),
        check_vma=False,
    )
```

time: 68.7 us -> 62.4 us (0.908)
  local copies, waits for them, and re-layouts: 3.54 us -> 0.02 us
  Pallas kernels: 64.4 us -> 61.6 us
    unnamed x8, local copies, waits for them, and re-layouts: 3.54 us -> 0.02 us
    pallas_call x1, Pallas kernels: 2.6 us -> 1.16 us  [local_stack(): pl.pallas_call(_head, name='head', out_shape=(jax.ShapeDtypeStruct((rows,...]
    pallas_call x1, Pallas kernels: 61.8 us -> 60.4 us  [local_stack(): pl.pallas_call(functools.partial(_kernel, n_sp, repeats, cycle, rows), na...]
where the time goes in v3:
time: 62.4 us; the launch traced here: 62.3 us
  Pallas kernels  61.6 us (99%)
  between operations  0.7 us (1%)
    pallas_call x1, Pallas kernels, local_stack(): pl.pallas_call(functools.partial(_kernel, n_sp, repeats, cycle, rows), na...  60.4 us

profile of v3, /device:TPU:7, one launch (start us, length us, event | category | flops | bytes accessed | tf_op | source)
XLA Modules:
  0.0 62.3 jit_solution(14836322168771556168)
XLA Ops:
  0.6 0.0 copy-start
  0.6 0.0 copy-start.1
  0.7 0.0 copy-start.2
  0.7 0.0 copy-start.3
  0.7 60.4 %stack.1 = (f32[512,256]{1,0:T(8,128)S(1)}, bf16[512,512]{1,0:T(8,128)(2,1)S(1)}) custom-call(bf16[512,512]{1,0:T(8,128)(2,1)} %x_ref.1, bf16[30,512,1024]{2,1,0:T(8,128)(2,1)} %bitcast.9, bf16[30,512,1024]{2,1,0:T(8,128)(2,1)} %bitcast.10, f32[10,3,1024]{2,1,0:T(4,128)} %bitcast.13, bf16[30,512,512]{2,1,0:T(8,128)(2,1)} %bitcast.11, ...), custom_call_target="tpu_custom_call" | custom-call | tf_op jit(solution)/shard_map/stack/pallas_call | solution.py:188
  61.1 0.0 copy-done
  61.1 0.0 copy-done.1
  61.1 0.0 copy-done.2
  61.1 0.0 copy-done.3
  61.2 1.2 %head.1 = (f32[512,256]{1,0:T(8,128)}, bf16[512,512]{1,0:T(8,128)(2,1)}) custom-call(f32[512,256]{1,0:T(8,128)S(1)} %get-tuple-element.4.skip, bf16[512,512]{1,0:T(8,128)(2,1)S(1)} %get-tuple-element.5.h_ref, bf16[256,256]{1,0:T(8,128)(2,1)S(1)} %copy-done, f32[1,256]{1,0:T(1,128)S(1)} %bitcast.7, bf16[256,256]{1,0:T(8,128)(2,1)S(1)} %copy-done.1, ...), custom_call_target="tpu_custom_call" | custom-call | tf_op jit(solution)/shard_map/head/pallas_call | solution.py:211
Async XLA Ops:
  0.6 60.5 %copy-start = (bf16[256,256]{1,0:T(8,128)(2,1)S(1)}, bf16[256,256]{1,0:T(8,128)(2,1)}, u32[]{:S(2)}) copy-start(bf16[256,256]{1,0:T(8,128)(2,1)} %w1_ref.1) | copy-start | bytes 393220
  0.6 60.5 %copy-start.1 = (bf16[256,256]{1,0:T(8,128)(2,1)S(1)}, bf16[256,256]{1,0:T(8,128)(2,1)}, u32[]{:S(2)}) copy-start(bf16[256,256]{1,0:T(8,128)(2,1)} %w2_ref.1) | copy-start | bytes 393220
  0.7 60.5 %copy-start.2 = (f32[256]{0:T(256)S(1)}, f32[256]{0:T(256)}, u32[]{:S(2)}) copy-start(f32[256]{0:T(256)} %param.17) | copy-start | bytes 3076
  0.7 60.5 %copy-start.3 = (f32[256]{0:T(256)S(1)}, f32[256]{0:T(256)}, u32[]{:S(2)}) copy-start(f32[256]{0:T(256)} %param.19) | copy-start | bytes 3076

commit v4 on v3

--- a/solution.py
+++ b/solution.py
@@ -10,8 +10,6 @@
 TILE = 16
 SLOTS = 5
 SIDE = 256
-SPLIT = (0, 1, 2, 3, 4, 5, 6, 7, 8, 9)
-EARLY = 0
 
 
 def _kernel(n_sp, repeats, cycle, rows, x_ref, wp_ref, wn_ref, b_ref, wr_ref, ws_ref,
@@ -54,12 +52,12 @@
             def fetch():
                 for c in weight_copies(layer + SLOTS - 1, (k + SLOTS - 1) % SLOTS):
                     c.start()
-            if k + SLOTS - 1 < cycle:
-                fetch()
-            else:
-                pl.when(s < repeats - 1)(fetch)
-            for c in weight_copies(layer, slot):
-                c.wait()
+            def always(ahead, f):
+                f() if k + ahead < cycle else pl.when(s < repeats - 1)(f)
+
+            def arrive():
+                for c in weight_copies(layer + 1, (k + 1) % SLOTS):
+                    c.wait()
 
             def both(buf, j):
                 ca, ct = j * SIDE, gate + j * SIDE
@@ -68,12 +66,12 @@
             def now(lo, n, j):
                 return jnp.dot(old[pad + lo:pad + lo + n, :], both(wnb, j), preferred_element_type=jnp.float32)
 
-            def past(lo, n, j):
+            def past(lo, n, w):
                 if d < TILE:
                     rows_in = old[pad + lo - TILE:pad + lo + n, :][TILE - d:TILE - d + n, :]
                 else:
                     rows_in = old[pad + lo - d:pad + lo - d + n, :]
-                return jnp.dot(rows_in, both(wpb, j), preferred_element_type=jnp.float32)
+                return jnp.dot(rows_in, w, preferred_element_type=jnp.float32)
 
             def gated(lo, n, j, z):
                 ca, ct = j * SIDE, gate + j * SIDE
@@ -85,34 +83,24 @@
                 res = jnp.dot(g_s[lo:lo + n, :], wrb[slot], preferred_element_type=jnp.float32)
                 new[new_pad + lo:new_pad + lo + n, :] = (old[pad + lo:pad + lo + n, :].astype(jnp.float32) + res).astype(new.dtype)
 
-            if k in SPLIT:
-                zn = [now(half, half, j) for j in range(2)]
-                if d > half:
-                    receive(0)
-                for j in range(2):
-                    gated(half, half, j, past(half, half, j) + zn[j])
-                residual(half, half)
-                zn = [now(0, half, j) for j in range(2)]
-                send(0)
-                receive(1 if d > half else 0)
-                for j in range(2):
-                    gated(0, half, j, past(0, half, j) + zn[j])
-                residual(0, half)
-                for lo in (half, 0):
-                    skip[lo:lo + half, :] += jnp.dot(g_s[lo:lo + half, :], wsb[slot], preferred_element_type=jnp.float32)
-                if new_pad > half:
-                    send(1)
-            else:
-                zn = [now(0, rows, j) for j in range(EARLY if k == cycle - 1 else 0)]
-                for i in range(2 if d > half else 1):
-                    receive(i)
-                for j in range(2):
-                    gated(0, rows, j, past(0, rows, j) + (zn[j] if j < len(zn) else now(0, rows, j)))
-                residual(0, rows)
-                for lo in (half, 0):
-                    skip[lo:lo + half, :] += jnp.dot(g_s[lo:lo + half, :], wsb[slot], preferred_element_type=jnp.float32)
-                for i in range(2 if new_pad > half else 1):
-                    send(i)
+            zn = [now(half, half, j) for j in range(2)]
+            if d > half:
+                receive(0)
+            for j in range(2):
+                gated(half, half, j, past(half, half, both(wpb, j)) + zn[j])
+            residual(half, half)
+            zn = [now(0, half, j) for j in range(2)]
+            send(0)
+            always(SLOTS - 1, fetch)
+            receive(1 if d > half else 0)
+            always(1, arrive)
+            for j in range(2):
+                gated(0, half, j, past(0, half, both(wpb, j)) + zn[j])
+            residual(0, half)
+            for lo in (half, 0):
+                skip[lo:lo + half, :] += jnp.dot(g_s[lo:lo + half, :], wsb[slot], preferred_element_type=jnp.float32)
+            if new_pad > half:
+                send(1)
         return carry
 
     x_copy = pltpu.make_async_copy(x_ref, hb[0].at[0, pads[0]:pads[0] + rows, :], xsem)
@@ -145,6 +133,8 @@
         pl.semaphore_wait(barrier, 1)
         halo_copies(0, 0)[0].start()
     b_copy.wait()
+    for c in first:
+        c.wait()
     lax.fori_loop(0, repeats, stack, 0)
     h_ref[...] = hb[0][repeats, pads[0]:pads[0] + rows, :]
 

time: 62.4 us -> 61 us (0.978)
  Pallas kernels: 61.6 us -> 60.2 us
    pallas_call x1, Pallas kernels: 60.4 us -> 59.1 us  [local_stack(): pl.pallas_call(functools.partial(_kernel, n_sp, repeats, cycle, rows), na...]
where the time goes in v4:
time: 61 us; the launch traced here: 60.9 us
  Pallas kernels  60.2 us (99%)
  between operations  0.7 us (1%)
    pallas_call x1, Pallas kernels, local_stack(): pl.pallas_call(functools.partial(_kernel, n_sp, repeats, cycle, rows), na...  59.1 us

profile of v4, /device:TPU:7, one launch (start us, length us, event | category | flops | bytes accessed | tf_op | source)
XLA Modules:
  0.0 60.9 jit_solution(3522466840988949367)
XLA Ops:
  0.6 0.0 copy-start
  0.6 0.0 copy-start.1
  0.7 0.0 copy-start.2
  0.7 0.0 copy-start.3
  0.7 59.1 %stack.1 = (f32[512,256]{1,0:T(8,128)S(1)}, bf16[512,512]{1,0:T(8,128)(2,1)S(1)}) custom-call(bf16[512,512]{1,0:T(8,128)(2,1)} %x_ref.1, bf16[30,512,1024]{2,1,0:T(8,128)(2,1)} %bitcast.9, bf16[30,512,1024]{2,1,0:T(8,128)(2,1)} %bitcast.10, f32[10,3,1024]{2,1,0:T(4,128)} %bitcast.13, bf16[30,512,512]{2,1,0:T(8,128)(2,1)} %bitcast.11, ...), custom_call_target="tpu_custom_call" | custom-call | tf_op jit(solution)/shard_map/stack/pallas_call | solution.py:178
  59.7 0.0 copy-done
  59.7 0.0 copy-done.1
  59.8 0.0 copy-done.2
  59.8 0.0 copy-done.3
  59.8 1.2 %head.1 = (f32[512,256]{1,0:T(8,128)}, bf16[512,512]{1,0:T(8,128)(2,1)}) custom-call(f32[512,256]{1,0:T(8,128)S(1)} %get-tuple-element.4.skip, bf16[512,512]{1,0:T(8,128)(2,1)S(1)} %get-tuple-element.5.h_ref, bf16[256,256]{1,0:T(8,128)(2,1)S(1)} %copy-done, f32[1,256]{1,0:T(1,128)S(1)} %bitcast.7, bf16[256,256]{1,0:T(8,128)(2,1)S(1)} %copy-done.1, ...), custom_call_target="tpu_custom_call" | custom-call | tf_op jit(solution)/shard_map/head/pallas_call | solution.py:201
Async XLA Ops:
  0.6 59.1 %copy-start = (bf16[256,256]{1,0:T(8,128)(2,1)S(1)}, bf16[256,256]{1,0:T(8,128)(2,1)}, u32[]{:S(2)}) copy-start(bf16[256,256]{1,0:T(8,128)(2,1)} %w1_ref.1) | copy-start | bytes 393220
  0.6 59.1 %copy-start.1 = (bf16[256,256]{1,0:T(8,128)(2,1)S(1)}, bf16[256,256]{1,0:T(8,128)(2,1)}, u32[]{:S(2)}) copy-start(bf16[256,256]{1,0:T(8,128)(2,1)} %w2_ref.1) | copy-start | bytes 393220
  0.7 59.1 %copy-start.2 = (f32[256]{0:T(256)S(1)}, f32[256]{0:T(256)}, u32[]{:S(2)}) copy-start(f32[256]{0:T(256)} %param.17) | copy-start | bytes 3076
  0.7 59.1 %copy-start.3 = (f32[256]{0:T(256)S(1)}, f32[256]{0:T(256)}, u32[]{:S(2)}) copy-start(f32[256]{0:T(256)} %param.19) | copy-start | bytes 3076
